TPU v7x, 32 devices: a whole 2x2x4 slice. The times are simulated.
32 devices in a mesh: rows: 8 (over z, x), cols: 4 (over y, core).
Axes of the slice: x: 2, y: 2, z: 4, core: 2. Of those that a mesh axis runs over, the one named last changes fastest.
Arguments:
- margins: bfloat16 [8192, 2048], P(('rows', 'cols')), may hold values from -512 to 512
- subset_masks: bfloat16 [8192, 8192], P('rows'), may hold values from 0 to 1
- ridge_param: float32 [], replicated, may hold values from 1024 to 4096
Outputs:
- weights: float32 [8192, 2048], P('rows', 'cols')
- residual_norm: float32 [2048], P('cols')
All inputs are finite; a program needn't handle non-finite values.
Results may differ from a plain program's by a relative error of at most 0.0021.
Values may be sent and summed in bfloat16 or wider, within the bound.
No kernel may reach another device: no remote copies, remote signals or barrier semaphores. Data moves between devices by JAX's collectives and lax.ppermute only.
A program may use at most 128 MiB of HBM per device.

v0:
```python
import jax
import jax.numpy as jnp
from jax import lax
from jax.sharding import PartitionSpec as P

ITERS = 2


def per_device(margins, subset_masks, ridge_param):
    design = subset_masks * 2 - 1
    regrouped = lax.all_to_all(margins, "cols", split_axis=1, concat_axis=0, tiled=True)

    def design_times(operand):
        return lax.dot_general(
            design, operand, (((0,), (0,)), ((), ())), preferred_element_type=jnp.float32
        )

    target = lax.psum_scatter(design_times(regrouped), "rows", scatter_dimension=0, tiled=True)
    first_norms = lax.psum(jnp.sum(target * target, axis=0), "rows")
    weights = jnp.zeros_like(target)
    residual = target
    direction = target
    norm_now = first_norms
    for iteration in range(ITERS):
        dir_low = direction.astype(jnp.bfloat16)
        fitted = jnp.dot(
            design,
            lax.all_gather(dir_low, "rows", axis=0, tiled=True),
            preferred_element_type=jnp.float32,
        )
        fitted_low = fitted.astype(jnp.bfloat16)
        partial_sum = jnp.sum(fitted * fitted_low.astype(jnp.float32), axis=0)
        partial_sum = partial_sum + ridge_param * jnp.sum(
            dir_low.astype(jnp.float32) * direction, axis=0
        )
        curvature = lax.psum(partial_sum, "rows")
        image = (
            lax.psum_scatter(design_times(fitted_low), "rows", scatter_dimension=0, tiled=True)
            + ridge_param * direction
        )
        alpha = norm_now / curvature
        weights = weights + alpha * direction
        residual = residual - alpha * image
        norm_next = lax.psum(jnp.sum(residual * residual, axis=0), "rows")
        if iteration + 1 < ITERS:
            direction = residual + norm_next / norm_now * direction
        norm_now = norm_next
    return (weights, jnp.sqrt(norm_now / first_norms))


def solution(mesh):
    in_specs = (P(("rows", "cols"), None), P("rows", None), P())
    out_specs = (P("rows", "cols"), P("cols"))
    return jax.shard_map(
        per_device, mesh=mesh, in_specs=in_specs, out_specs=out_specs, check_vma=False
    )
```

profile of v0, /device:TPU:0, one launch (start us, length us, event | category | flops | bytes accessed | tf_op | source)
XLA Modules:
  0.0 1246.0 jit_solution(5039856017839600145)
XLA Ops:
  7.2 0.0 reduce-scatter.4.cloned.1.call-start
  7.2 1.5 copy.5
  8.7 18.5 %all_to_all.19 = bf16[256,4,512]{0,2,1:T(8,128)(2,1)S(1)} all-to-all(bf16[256,4,512]{0,2,1:T(8,128)(2,1)S(1)} %bitcast.9), channel_id=1, replica_groups=mesh['rows'=8,'cols'=4] {'cols'}, dimensions={1} | all-to-all | bytes 2097152 | tf_op jit(solution)/shard_map/all_to_all | solution.py:11
  27.2 0.5 copy.6
  27.7 15.7 %fusion.4 = f32[8192,512]{1,0:T(8,128)} fusion(bf16[1024,512]{1,0:T(8,128)(2,1)S(1)} %bitcast.10, bf16[1024,8192]{1,0:T(8,128)(2,1)} %param.4), kind=kOutput, calls=%fused_computation.15 | convolution fusion | flops 8606711808 | bytes 34603008 | tf_op jit(solution)/shard_map/dot_general | solution.py:14
  43.5 0.0 reduce-scatter.4.cloned.1.call-update
  43.5 0.0 all-gather.3.cloned.1.call-start
  43.6 279.9 %reduce-scatter.4.cloned.1.call-done = f32[1024,512]{1,0:T(8,128)} async-done(((f32[8192,512]{1,0:T(8,128)}), f32[1024,512]{1,0:T(8,128)}) %reduce-scatter.4.cloned.1.call-update) | async-done | bytes 2097168 | tf_op jit(solution)/shard_map/reduce_scatter | solution.py:18
  323.5 3.6 multiply_reduce_fusion.4
  327.1 0.0 all-gather.3.cloned.1.call-update
  327.1 0.2 reduce-scatter.6.cloned.1.call-start
  327.4 123.5 %all-gather.3.cloned.1.call-done = bf16[8192,512]{1,0:T(8,128)(2,1)} async-done(((bf16[1024,512]{1,0:T(8,128)(2,1)}), bf16[8192,512]{1,0:T(8,128)(2,1)}) %all-gather.3.cloned.1.call-update) | async-done | bytes 8388624 | tf_op jit(solution)/shard_map/all_gather | solution.py:28
  450.8 14.8 %multiply_reduce_fusion.5 = (f32[512]{0:T(512)S(1)}, bf16[1024,512]{1,0:T(8,128)(2,1)S(1)}) fusion(bf16[8192,512]{1,0:T(8,128)(2,1)} %all-gather.3.cloned.1.call-done, bf16[1024,8192]{1,0:T(8,128)(2,1)} %param.4), kind=kOutput, calls=%fused_computation.9 | convolution fusion | flops 8609333248 | bytes 26216448 | tf_op jit(solution)/shard_map/dot_general | solution.py:26
  465.6 15.7 %fusion.2 = f32[8192,512]{1,0:T(8,128)} fusion(bf16[1024,8192]{1,0:T(8,128)(2,1)} %param.4, bf16[1024,512]{1,0:T(8,128)(2,1)S(1)} %get-tuple-element.12), kind=kOutput, calls=%fused_computation.13 | convolution fusion | flops 8606711808 | bytes 34603008 | tf_op jit(solution)/shard_map/dot_general | solution.py:14
  481.4 0.0 reduce-scatter.6.cloned.1.call-update
  481.4 0.0 all-gather.5.cloned.1.call-start
  482.3 19.3 %all-reduce = (f32[512]{0:T(512)S(1)}, f32[512]{0:T(512)S(1)}) all-reduce(f32[512]{0:T(512)S(1)} %get-tuple-element.3, f32[512]{0:T(512)S(1)} %multiply_add_fusion.9), channel_id=1, replica_groups=mesh['rows'=8,'cols'=4] {'rows'}, use_global_device_ids=true, to_apply=%region_2.0 | all-reduce | flops 1024 | bytes 8192 | tf_op jit(solution)/shard_map/psum | solution.py:19
  501.5 258.0 %reduce-scatter.6.cloned.1.call-done = f32[1024,512]{1,0:T(8,128)} async-done(((f32[8192,512]{1,0:T(8,128)}), f32[1024,512]{1,0:T(8,128)}) %reduce-scatter.6.cloned.1.call-update) | async-done | bytes 2097168 | tf_op jit(solution)/shard_map/reduce_scatter | solution.py:38
  759.5 2.0 multiply_reduce_fusion.3
  761.6 19.5 %psum.37 = f32[512]{0:T(512)S(1)} all-reduce(f32[512]{0:T(512)S(1)} %multiply_reduce_fusion.3), channel_id=1, replica_groups=mesh['rows'=8,'cols'=4] {'rows'}, use_global_device_ids=true, to_apply=%region_8.0 | all-reduce | flops 512 | bytes 4096 | tf_op jit(solution)/shard_map/psum | solution.py:44
  781.0 3.2 multiply_reduce_fusion.1
  784.2 0.0 all-gather.5.cloned.1.call-update
  784.2 0.3 reduce-scatter.8.cloned.1.call-start
  784.5 121.6 %all-gather.5.cloned.1.call-done = bf16[8192,512]{1,0:T(8,128)(2,1)} async-done(((bf16[1024,512]{1,0:T(8,128)(2,1)}), bf16[8192,512]{1,0:T(8,128)(2,1)}) %all-gather.5.cloned.1.call-update) | async-done | bytes 8388624 | tf_op jit(solution)/shard_map/all_gather | solution.py:28
  906.1 14.8 %multiply_reduce_fusion.2 = (f32[512]{0:T(512)S(1)}, bf16[1024,512]{1,0:T(8,128)(2,1)S(1)}) fusion(bf16[8192,512]{1,0:T(8,128)(2,1)} %all-gather.5.cloned.1.call-done, bf16[1024,8192]{1,0:T(8,128)(2,1)} %param.4), kind=kOutput, calls=%fused_computation.4 | convolution fusion | flops 8609333248 | bytes 26216448 | tf_op jit(solution)/shard_map/dot_general | solution.py:26
  920.9 15.7 %fusion = f32[8192,512]{1,0:T(8,128)} fusion(bf16[1024,8192]{1,0:T(8,128)(2,1)} %param.4, bf16[1024,512]{1,0:T(8,128)(2,1)S(1)} %get-tuple-element.14), kind=kOutput, calls=%fused_computation.11 | convolution fusion | flops 8606711808 | bytes 34603008 | tf_op jit(solution)/shard_map/dot_general | solution.py:14
  936.6 0.0 reduce-scatter.8.cloned.1.call-update
  936.7 19.3 %psum.38 = f32[512]{0:T(512)S(1)} all-reduce(f32[512]{0:T(512)S(1)} %multiply_add_fusion.8), channel_id=1, replica_groups=mesh['rows'=8,'cols'=4] {'rows'}, use_global_device_ids=true, to_apply=%region_11.0 | all-reduce | flops 512 | bytes 4096 | tf_op jit(solution)/shard_map/psum | solution.py:36
  956.0 258.9 %reduce-scatter.8.cloned.1.call-done = f32[1024,512]{1,0:T(8,128)} async-done(((f32[8192,512]{1,0:T(8,128)}), f32[1024,512]{1,0:T(8,128)}) %reduce-scatter.8.cloned.1.call-update) | async-done | bytes 2097168 | tf_op jit(solution)/shard_map/reduce_scatter | solution.py:38
  1214.9 4.6 multiply_reduce_fusion
  1219.4 19.5 %psum.39 = f32[512]{0:T(512)S(1)} all-reduce(f32[512]{0:T(512)S(1)} %get-tuple-element.7), channel_id=1, replica_groups=mesh['rows'=8,'cols'=4] {'rows'}, use_global_device_ids=true, to_apply=%region_14.0 | all-reduce | flops 512 | bytes 4096 | tf_op jit(solution)/shard_map/psum | solution.py:44
  1238.9 0.6 divide_sqrt_fusion
  (7 shorter events, 0.0 us)
Async XLA Ops:
  7.2 316.3 %reduce-scatter.4.cloned.1.call-start = ((), (), s32[]{:S(2)}) async-start(), calls=%async_computation.4 | async-start | bytes 18874368 | tf_op jit(solution)/shard_map/reduce_scatter | solution.py:18
  43.5 407.3 %all-gather.3.cloned.1.call-start = ((), (), s32[]{:S(2)}) async-start(), calls=%async_computation.5 | async-start | bytes 9437184 | tf_op jit(solution)/shard_map/all_gather | solution.py:28
  327.1 432.4 %reduce-scatter.6.cloned.1.call-start = ((), (), s32[]{:S(2)}) async-start(), calls=%async_computation.6 | async-start | bytes 18874368 | tf_op jit(solution)/shard_map/reduce_scatter | solution.py:38
  481.4 278.1 %copy-start = (f32[1024,512]{1,0:T(8,128)S(1)}, f32[1024,512]{1,0:T(8,128)}, u32[]{:S(2)}) copy-start(f32[1024,512]{1,0:T(8,128)} %reduce-scatter.4.cloned.1.call-done) | copy-start | bytes 6291460
  481.4 424.7 %all-gather.5.cloned.1.call-start = ((), (), s32[]{:S(2)}) async-start(), calls=%async_computation.7 | async-start | bytes 9437184 | tf_op jit(solution)/shard_map/all_gather | solution.py:28
  784.2 430.7 %reduce-scatter.8.cloned.1.call-start = ((), (), s32[]{:S(2)}) async-start(), calls=%async_computation.8 | async-start | bytes 18874368 | tf_op jit(solution)/shard_map/reduce_scatter | solution.py:38
Sparse Core Ops, SparseCore 0:
  43.6 279.8 reduce-scatter.3
  327.2 123.5 all-gather.2
  481.5 277.9 reduce-scatter.5
  784.3 121.7 all-gather.4
  936.8 278.0 reduce-scatter.7
where the time goes:
time: 1250 us
  waiting for transfers between devices  1040 us (83%)
  blocking collectives  96 us (8%)
  matrix products  76.8 us (6%)
  between operations  14.6 us (1%)
  other arithmetic  14 us (1%)
    reduce_scatter x2, waiting for transfers between devices, per_device(): lax.psum_scatter(design_times(fitted_low), 'rows', scatter_dimension=0, t...  517 us
    reduce_scatter x1, waiting for transfers between devices, per_device(): lax.psum_scatter(design_times(regrouped), 'rows', scatter_dimension=0, ti...  280 us
    all_gather x2, waiting for transfers between devices, per_device(): lax.all_gather(dir_low, 'rows', axis=0, tiled=True)  245 us
    dot_general x3, matrix products, design_times(): lax.dot_general(design, operand, (((0,), (0,)), ((), ())), preferred_elem...  47.2 us
    psum x2, blocking collectives, per_device(): norm_next = lax.psum(jnp.sum(residual * residual, axis=0), 'rows')  38.9 us
    dot_general x2, matrix products, per_device(): jnp.dot(design, lax.all_gather(dir_low, 'rows', axis=0, tiled=True), pref...  29.6 us
  transfers between devices with their start and end apart: 5, of which 5 were waited for; matrix products, arithmetic and copies ran while one was open for 0% of the time, Pallas kernels for 0%

commit v1 on v0

v1 whole, which is shorter than its diff:
```python
import jax
import jax.numpy as jnp
from jax import lax
from jax.sharding import PartitionSpec as P


GROUPS = 2
CHAINS = 2
HEADROOM = 32768.0


def ring_block(position, size):
    return jnp.where(position < size // 2, 2 * position, 2 * (size - 1 - position) + 1)


def ring_position(block, size):
    return jnp.where(block % 2 == 0, block // 2, size - 1 - block // 2)


def ring_order(size):
    return [2 * q if q < size // 2 else 2 * (size - 1 - q) + 1 for q in range(size)]


def make_body(rows_size, cols_size):
    order = ring_order(rows_size)
    up = [(order[q], order[(q + 1) % rows_size]) for q in range(rows_size)]
    down = [(b, a) for a, b in up]
    perms = (up, down)

    def total(x, axis, size):
        step = 1
        while step < size:
            x = x + lax.ppermute(x, axis, [(i, i ^ step) for i in range(size)])
            step *= 2
        return x

    def per_device(margins, subset_masks, ridge_param):
        local_subsets, n = subset_masks.shape
        piece, e = margins.shape
        subsets = local_subsets * rows_size
        columns = e // cols_size
        width = columns // GROUPS
        block = n // rows_size
        chain = block // CHAINS
        me = lax.axis_index("rows")
        position = ring_position(me, rows_size)
        mycol = lax.axis_index("cols")
        groups = range(GROUPS)
        blocks = [ring_block((position + j) % rows_size, rows_size) for j in range(rows_size)]

        sizes = jnp.sum(jnp.abs(margins.astype(jnp.float32)), axis=0, keepdims=True)
        l1 = None
        for step in range(cols_size):
            sent = lax.dynamic_slice(sizes, (0, (mycol ^ step) * columns), (1, columns))
            if step:
                sent = lax.ppermute(sent, "cols", [(i, i ^ step) for i in range(cols_size)])
            l1 = sent if l1 is None else l1 + sent
        target_bound = jnp.maximum(total(l1, "rows", rows_size) * 1.01, 1e-30)

        regrouped = jnp.zeros((local_subsets, columns), margins.dtype)
        for step in range(cols_size):
            other = mycol ^ step
            sent = lax.dynamic_slice(margins, (0, other * columns), (piece, columns))
            if step:
                sent = lax.ppermute(sent, "cols", [(i, i ^ step) for i in range(cols_size)])
            regrouped = lax.dynamic_update_slice(regrouped, sent, (other * piece, 0))

        design = lax.optimization_barrier(subset_masks * 2 - 1)

        def design_rows(b, c, early=False):
            at = (0, b * block + c * chain)
            if early:
                return lax.dynamic_slice(subset_masks, at, (local_subsets, chain)) * 2 - 1
            return lax.dynamic_slice(design, at, (local_subsets, chain))

        def group_of(x, g):
            return x[:, g * width : (g + 1) * width]

        def scatter_sums(operands, bounds, early=0):
            scale = [HEADROOM / b for b in bounds]
            inverse = [b * (1.0 / HEADROOM) for b in bounds]

            def partial(g, c, s, b):
                return lax.dot_general(
                    design_rows(b, c, s < early), operands[g], (((0,), (0,)), ((), ())),
                    preferred_element_type=jnp.float32,
                )

            keys = [(g, c) for c in range(CHAINS) for g in range(GROUPS)]
            held = {}
            for s in range(rows_size):
                for g, c in keys:
                    j = (rows_size - 1 - s) if g == 0 else (s + 1) % rows_size
                    value = partial(g, c, s, blocks[j])
                    scale[g], inverse[g] = lax.optimization_barrier((scale[g], inverse[g]))
                    if s:
                        value = value + held[g, c].astype(jnp.float32) * inverse[g]
                    if s < rows_size - 1:
                        value = (value * scale[g]).astype(jnp.float16)
                        value = lax.ppermute(value, "rows", perms[g])
                    held[g, c] = value
            return [jnp.concatenate([held[g, c] for c in range(CHAINS)], axis=0) for g in range(GROUPS)]

        def gather_times(lows):
            keys = [(g, c) for c in range(CHAINS) for g in range(GROUPS)]
            held = {(g, c): lows[g][c * chain : (c + 1) * chain] for g, c in keys}
            result = [None] * GROUPS
            for s in range(rows_size):
                following = {}
                for g, c in keys:
                    if s < rows_size - 1:
                        following[g, c] = lax.ppermute(held[g, c], "rows", perms[g])
                for g, c in keys:
                    j = (rows_size - s) % rows_size if g == 0 else s
                    product = jnp.dot(
                        design_rows(blocks[j], c), held[g, c], preferred_element_type=jnp.float32
                    )
                    result[g] = product if result[g] is None else result[g] + product
                held = following
            return result

        def column_sum(x):
            return jnp.sum(x, axis=0, keepdims=True)

        target = scatter_sums(
            [group_of(regrouped, g) for g in groups], [group_of(target_bound, g) for g in groups],
            early=2,
        )
        first_norms = [total(column_sum(t * t), "rows", rows_size) for t in target]
        lows = [t.astype(jnp.bfloat16) for t in target]
        fitted0 = gather_times(lows)
        fitted_low = [f.astype(jnp.bfloat16) for f in fitted0]
        curvature = [
            total(
                column_sum(fitted0[g] * fitted_low[g].astype(jnp.float32))
                + ridge_param * column_sum(lows[g].astype(jnp.float32) * target[g]),
                "rows", rows_size,
            )
            for g in groups
        ]
        gain = 1.02 * subsets * float(n) ** 0.5
        image = scatter_sums(
            fitted_low, [jnp.maximum(gain * jnp.sqrt(v), 1e-30) for v in first_norms]
        )
        alpha0 = [first_norms[g] / curvature[g] for g in groups]
        residual = [
            target[g] - alpha0[g] * (image[g] + ridge_param * target[g]) for g in groups
        ]
        norm1 = [total(column_sum(r * r), "rows", rows_size) for r in residual]
        beta = [norm1[g] / first_norms[g] for g in groups]
        direction = [residual[g] + beta[g] * target[g] for g in groups]
        fresh = gather_times([r.astype(jnp.bfloat16) for r in residual])
        fitted1 = [fresh[g] + beta[g] * fitted0[g] for g in groups]
        fitted_low = [f.astype(jnp.bfloat16) for f in fitted1]
        curvature = [
            total(
                column_sum(fitted1[g] * fitted_low[g].astype(jnp.float32))
                + ridge_param * column_sum(direction[g] * direction[g]),
                "rows", rows_size,
            )
            for g in groups
        ]
        direction_norm = [norm1[g] + beta[g] * beta[g] * first_norms[g] for g in groups]
        image = scatter_sums(
            fitted_low, [jnp.maximum(1.5 * gain * jnp.sqrt(v), 1e-30) for v in direction_norm]
        )
        alpha1 = [norm1[g] / curvature[g] for g in groups]
        weights = jnp.concatenate(
            [alpha0[g] * target[g] + alpha1[g] * direction[g] for g in groups], axis=1
        )
        residual = [
            residual[g] - alpha1[g] * (image[g] + ridge_param * direction[g]) for g in groups
        ]
        last = jnp.concatenate([column_sum(r * r) for r in residual], axis=1)
        last = total(last, "rows", rows_size)
        ratio = last / jnp.concatenate(first_norms, axis=1)
        return weights, jnp.sqrt(ratio).reshape(columns)

    return per_device


def solution(mesh):
    in_specs = (P(("rows", "cols"), None), P("rows", None), P())
    out_specs = (P("rows", "cols"), P("cols"))
    body = make_body(mesh.shape["rows"], mesh.shape["cols"])

    return jax.shard_map(body, mesh=mesh, in_specs=in_specs, out_specs=out_specs, check_vma=False)
```

time: 1250 us -> 524 us (0.42)
  waiting for transfers between devices: 1040 us -> 197 us
  starting transfers between devices: 0.61 us -> 200 us
  blocking collectives: 96 us -> 0 us
    reduce_scatter x3 -> x0, waiting for transfers between devices: 797 us -> none  [the longest x2 517 us: per_device(): lax.psum_scatter(design_times(fitted_low), 'rows', scatter_dimension=0, t...]
    all_gather x2 -> x0, waiting for transfers between devices: 245 us -> none  [per_device(): lax.all_gather(dir_low, 'rows', axis=0, tiled=True)]
    ppermute x0 -> x176, starting transfers between devices: none -> 200 us  [the longest x84 93.9 us: scatter_sums(): value = lax.ppermute(value, 'rows', perms[g])]
    ppermute x0 -> x176, waiting for transfers between devices: none -> 197 us  [the longest x84 87.5 us: scatter_sums(): value = lax.ppermute(value, 'rows', perms[g])]
    psum x4 -> x0, blocking collectives: 77.5 us -> none  [the longest x2 38.9 us: per_device(): norm_next = lax.psum(jnp.sum(residual * residual, axis=0), 'rows')]
    all_to_all x1 -> x0, blocking collectives: 18.5 us -> none  [per_device(): lax.all_to_all(margins, 'cols', split_axis=1, concat_axis=0, tiled=True)]
    sub x0 -> x1, other arithmetic: none -> 14.1 us  [per_device(): design = lax.optimization_barrier(subset_masks * 2 - 1)]
    dot_general x5 -> x160, matrix products: 76.8 us -> 87.8 us  [the longest x96 59.4 us: partial(): lax.dot_general(design_rows(b, c, s < early), operands[g], (((0,), (0,)),...]
  transfers between devices with their start and end apart: 5 -> 176, of which waited for: 5 -> 96; matrix products, arithmetic and copies ran while one was open for 0% -> 20% of each run, Pallas kernels for 0% -> 0%
where the time goes in v1:
time: 524 us; the launch traced here: 515 us
  starting transfers between devices  200 us (38%)
  waiting for transfers between devices  197 us (38%)
  matrix products  87.8 us (17%)
  other arithmetic  25.5 us (5%)
    ppermute x84, starting transfers between devices, scatter_sums(): value = lax.ppermute(value, 'rows', perms[g])  93.9 us
    ppermute x84, waiting for transfers between devices, scatter_sums(): value = lax.ppermute(value, 'rows', perms[g])  87.5 us
    ppermute x56, waiting for transfers between devices, gather_times(): following[g, c] = lax.ppermute(held[g, c], 'rows', perms[g])  72.5 us
    dot_general x96, matrix products, partial(): lax.dot_general(design_rows(b, c, s < early), operands[g], (((0,), (0,)),...  59.4 us
    ppermute x56, starting transfers between devices, gather_times(): following[g, c] = lax.ppermute(held[g, c], 'rows', perms[g])  58.1 us
    ppermute x30, starting transfers between devices, total(): x = x + lax.ppermute(x, axis, [(i, i ^ step) for i in range(size)])  42.6 us
    ppermute x30, waiting for transfers between devices, total(): x = x + lax.ppermute(x, axis, [(i, i ^ step) for i in range(size)])  36.6 us
    dot_general x64, matrix products, gather_times(): jnp.dot(design_rows(blocks[j], c), held[g, c], preferred_element_type=jnp...  28.4 us
  transfers between devices with their start and end apart: 176, of which 96 were waited for; matrix products, arithmetic and copies ran while one was open for 20% of the time, Pallas kernels for 0%

profile of v1, /device:TPU:0, one launch (start us, length us, event | category | flops | bytes accessed | tf_op | source)
XLA Modules:
  0.0 515.2 jit_solution(7197061172846087070)
XLA Ops:
  8.9 14.1 %multiply_add_fusion = bf16[1024,8192]{1,0:T(8,128)(2,1)} fusion(bf16[1024,8192]{1,0:T(8,128)(2,1)} %param.4), kind=kLoop, calls=%fused_computation | loop fusion | flops 16777216 | bytes 33554432 | tf_op jit(solution)/shard_map/sub | solution.py:68
  65.4 4.6 collective-permute-done.85
  78.0 3.2 collective-permute-done.86
  89.5 2.9 collective-permute-done.87
  101.0 2.9 collective-permute-done.88
  112.2 3.1 collective-permute-done.89
  129.1 4.2 collective-permute-done.91
  137.1 2.7 collective-permute-start.93
  143.7 3.2 collective-permute-done.94
  151.5 3.2 collective-permute-done.28
  158.1 3.0 collective-permute-done.96
  166.3 3.1 collective-permute-done.30
  172.9 3.0 collective-permute-done.98
  248.9 3.4 collective-permute-done.43
  253.9 3.9 collective-permute-done.50
  264.7 4.4 collective-permute-done.51
  276.0 4.3 collective-permute-done.52
  287.2 4.3 collective-permute-done.53
  311.5 3.9 collective-permute-done.56
  320.0 2.7 collective-permute-start.125
  322.7 3.0 collective-permute-start.58
  327.2 3.9 collective-permute-start.59
  341.6 4.4 collective-permute-done.61
  347.7 3.9 collective-permute-done.60
  358.9 3.9 collective-permute-done.62
  370.1 3.9 collective-permute-done.64
  395.4 4.5 collective-permute-done.70
  429.6 7.4 %collective-permute-done.142 = f32[1,256]{1,0:T(1,128)S(1)} collective-permute-done((f32[1,256]{1,0:T(1,128)S(1)}, f32[1,256]{1,0:T(1,128)S(1)}, u32[]{:S(2)}, u32[]{:S(2)}) %collective-permute-start.142) | collective-permute-done | bytes 1056 | tf_op jit(solution)/shard_map/ppermute | solution.py:33
  443.4 5.8 %collective-permute-done.144 = f32[1,256]{1,0:T(1,128)S(1)} collective-permute-done((f32[1,256]{1,0:T(1,128)S(1)}, f32[1,256]{1,0:T(1,128)S(1)}, u32[]{:S(2)}, u32[]{:S(2)}) %collective-permute-start.144) | collective-permute-done | bytes 1056 | tf_op jit(solution)/shard_map/ppermute | solution.py:33
  457.9 5.4 %collective-permute-done.153 = f16[512,256]{1,0:T(8,128)(2,1)S(1)} collective-permute-done((f16[512,256]{1,0:T(8,128)(2,1)S(1)}, f16[512,256]{1,0:T(8,128)(2,1)S(1)}, u32[]{:S(2)}, u32[]{:S(2)}) %collective-permute-start.153) | collective-permute-done | bytes 262176 | tf_op jit(solution)/shard_map/ppermute | solution.py:100
  496.3 2.7 collective-permute-done.158
  503.4 2.7 collective-permute-done.173
  (599 shorter events, 379.6 us)
Async XLA Ops:
  2.2 20.8 %collective-permute-start.3 = (f32[1,512]{1,0:T(1,128)S(1)}, f32[1,512]{1,0:T(1,128)S(1)}, u32[]{:S(2)}, u32[]{:S(2)}) collective-permute-start(f32[1,512]{1,0:T(1,128)S(1)} %bitcast.460), channel_id=1, source_target_pairs={{0,1},{1,0},{2,3},{3,2},{4,5},{5,4},{6,7},{7,6},{8,9},{9,8},{10,11... | collective-permute-start | bytes 6152 | tf_op jit(solution)/shard_map/ppermute | solution.py:56
  2.7 20.3 %collective-permute-start.4 = (f32[1,512]{1,0:T(1,128)S(1)}, f32[1,512]{1,0:T(1,128)S(1)}, u32[]{:S(2)}, u32[]{:S(2)}) collective-permute-start(f32[1,512]{1,0:T(1,128)S(1)} %bitcast.459), channel_id=1, source_target_pairs={{0,2},{1,3},{2,0},{3,1},{4,6},{5,7},{6,4},{7,5},{8,10},{9,11},{10,... | collective-permute-start | bytes 6152 | tf_op jit(solution)/shard_map/ppermute | solution.py:56
  5.3 17.7 %collective-permute-start.5 = (f32[1,512]{1,0:T(1,128)S(1)}, f32[1,512]{1,0:T(1,128)S(1)}, u32[]{:S(2)}, u32[]{:S(2)}) collective-permute-start(f32[1,512]{1,0:T(1,128)S(1)} %bitcast.458), channel_id=1, source_target_pairs={{0,3},{1,2},{2,1},{3,0},{4,7},{5,6},{6,5},{7,4},{8,11},{9,10},{10,... | collective-permute-start | bytes 6152 | tf_op jit(solution)/shard_map/ppermute | solution.py:56
  6.7 28.1 %collective-permute-start = (bf16[256,512]{1,0:T(8,128)(2,1)S(1)}, bf16[256,512]{1,0:T(8,128)(2,1)S(1)}, u32[]{:S(2)}, u32[]{:S(2)}) collective-permute-start(bf16[256,512]{1,0:T(8,128)(2,1)S(1)} %get-tuple-element.360), channel_id=1, source_target_pairs={{0,1},{1,0},{2,3},{3,2},{4,5},{5,4},{6,7},{7,6},{8,9},{9,8},{10,11... | collective-permute-start | bytes 786440 | tf_op jit(solution)/shard_map/ppermute | solution.py:65
  6.9 27.9 %collective-permute-start.1 = (bf16[256,512]{1,0:T(8,128)(2,1)S(1)}, bf16[256,512]{1,0:T(8,128)(2,1)S(1)}, u32[]{:S(2)}, u32[]{:S(2)}) collective-permute-start(bf16[256,512]{1,0:T(8,128)(2,1)S(1)} %get-tuple-element.359), channel_id=1, source_target_pairs={{0,2},{1,3},{2,0},{3,1},{4,6},{5,7},{6,4},{7,5},{8,10},{9,11},{10,... | collective-permute-start | bytes 786440 | tf_op jit(solution)/shard_map/ppermute | solution.py:65
  57.4 12.6 %collective-permute-start.85 = (f16[512,256]{1,0:T(8,128)(2,1)S(1)}, f16[512,256]{1,0:T(8,128)(2,1)S(1)}, u32[]{:S(2)}, u32[]{:S(2)}) collective-permute-start(f16[512,256]{1,0:T(8,128)(2,1)S(1)} %fusion.66), channel_id=1, source_target_pairs={{8,0},{16,8},{24,16},{28,24},{20,28},{12,20},{4,12},{0,4},{9,1},{1... | collective-permute-start | bytes 786440 | tf_op jit(solution)/shard_map/ppermute | solution.py:100
  62.5 12.4 %collective-permute-start.18 = (f16[512,256]{1,0:T(8,128)(2,1)S(1)}, f16[512,256]{1,0:T(8,128)(2,1)S(1)}, u32[]{:S(2)}, u32[]{:S(2)}) collective-permute-start(f16[512,256]{1,0:T(8,128)(2,1)S(1)} %fusion.79), channel_id=1, source_target_pairs={{0,8},{8,16},{16,24},{24,28},{28,20},{20,12},{12,4},{4,0},{1,9},{9... | collective-permute-start | bytes 786440 | tf_op jit(solution)/shard_map/ppermute | solution.py:100
  124.0 13.1 %collective-permute-start.27 = (bf16[512,256]{1,0:T(8,128)(2,1)S(1)}, bf16[512,256]{1,0:T(8,128)(2,1)S(1)}, u32[]{:S(2)}, u32[]{:S(2)}) collective-permute-start(bf16[512,256]{1,0:T(8,128)(2,1)S(1)} %get-tuple-element.365), channel_id=1, source_target_pairs={{0,8},{8,16},{16,24},{24,28},{28,20},{20,12},{12,4},{4,0},{1,9},{9... | collective-permute-start | bytes 786440 | tf_op jit(solution)/shard_map/ppermute | solution.py:112
  125.2 15.1 %collective-permute-start.26 = (bf16[512,256]{1,0:T(8,128)(2,1)S(1)}, bf16[512,256]{1,0:T(8,128)(2,1)S(1)}, u32[]{:S(2)}, u32[]{:S(2)}) collective-permute-start(bf16[512,256]{1,0:T(8,128)(2,1)S(1)} %get-tuple-element.364), channel_id=1, source_target_pairs={{0,8},{8,16},{16,24},{24,28},{28,20},{20,12},{12,4},{4,0},{1,9},{9... | collective-permute-start | bytes 786440 | tf_op jit(solution)/shard_map/ppermute | solution.py:112
  133.4 13.6 %collective-permute-start.94 = (bf16[512,256]{1,0:T(8,128)(2,1)S(1)}, bf16[512,256]{1,0:T(8,128)(2,1)S(1)}, u32[]{:S(2)}, u32[]{:S(2)}) collective-permute-start(bf16[512,256]{1,0:T(8,128)(2,1)S(1)} %get-tuple-element.368), channel_id=1, source_target_pairs={{8,0},{16,8},{24,16},{28,24},{20,28},{12,20},{4,12},{0,4},{9,1},{1... | collective-permute-start | bytes 786440 | tf_op jit(solution)/shard_map/ppermute | solution.py:112
  136.9 105.0 %collective-permute-start.25 = (f32[1,256]{1,0:T(1,128)S(1)}, f32[1,256]{1,0:T(1,128)S(1)}, u32[]{:S(2)}, u32[]{:S(2)}) collective-permute-start(f32[1,256]{1,0:T(1,128)S(1)} %add.1115), channel_id=1, source_target_pairs={{0,16},{4,20},{8,24},{12,28},{16,0},{20,4},{24,8},{28,12},{1,17},{... | collective-permute-start | bytes 3080 | tf_op jit(solution)/shard_map/ppermute | solution.py:33
  137.1 108.7 %collective-permute-start.93 = (f32[1,256]{1,0:T(1,128)S(1)}, f32[1,256]{1,0:T(1,128)S(1)}, u32[]{:S(2)}, u32[]{:S(2)}) collective-permute-start(f32[1,256]{1,0:T(1,128)S(1)} %add.1193), channel_id=1, source_target_pairs={{0,16},{4,20},{8,24},{12,28},{16,0},{20,4},{24,8},{28,12},{1,17},{... | collective-permute-start | bytes 3080 | tf_op jit(solution)/shard_map/ppermute | solution.py:33
  141.4 13.3 %collective-permute-start.28 = (bf16[512,256]{1,0:T(8,128)(2,1)S(1)}, bf16[512,256]{1,0:T(8,128)(2,1)S(1)}, u32[]{:S(2)}, u32[]{:S(2)}) collective-permute-start(bf16[512,256]{1,0:T(8,128)(2,1)S(1)} %collective-permute-done.26), channel_id=1, source_target_pairs={{0,8},{8,16},{16,24},{24,28},{28,20},{20,12},{12,4},{4,0},{1,9},{9... | collective-permute-start | bytes 786440 | tf_op jit(solution)/shard_map/ppermute | solution.py:112
  149.1 12.0 %collective-permute-start.96 = (bf16[512,256]{1,0:T(8,128)(2,1)S(1)}, bf16[512,256]{1,0:T(8,128)(2,1)S(1)}, u32[]{:S(2)}, u32[]{:S(2)}) collective-permute-start(bf16[512,256]{1,0:T(8,128)(2,1)S(1)} %collective-permute-done.94), channel_id=1, source_target_pairs={{8,0},{16,8},{24,16},{28,24},{20,28},{12,20},{4,12},{0,4},{9,1},{1... | collective-permute-start | bytes 786440 | tf_op jit(solution)/shard_map/ppermute | solution.py:112
  155.5 13.8 %collective-permute-start.30 = (bf16[512,256]{1,0:T(8,128)(2,1)S(1)}, bf16[512,256]{1,0:T(8,128)(2,1)S(1)}, u32[]{:S(2)}, u32[]{:S(2)}) collective-permute-start(bf16[512,256]{1,0:T(8,128)(2,1)S(1)} %collective-permute-done.28), channel_id=1, source_target_pairs={{0,8},{8,16},{16,24},{24,28},{28,20},{20,12},{12,4},{4,0},{1,9},{9... | collective-permute-start | bytes 786440 | tf_op jit(solution)/shard_map/ppermute | solution.py:112
  163.9 12.1 %collective-permute-start.98 = (bf16[512,256]{1,0:T(8,128)(2,1)S(1)}, bf16[512,256]{1,0:T(8,128)(2,1)S(1)}, u32[]{:S(2)}, u32[]{:S(2)}) collective-permute-start(bf16[512,256]{1,0:T(8,128)(2,1)S(1)} %collective-permute-done.96), channel_id=1, source_target_pairs={{8,0},{16,8},{24,16},{28,24},{20,28},{12,20},{4,12},{0,4},{9,1},{1... | collective-permute-start | bytes 786440 | tf_op jit(solution)/shard_map/ppermute | solution.py:112
  170.5 12.7 %collective-permute-start.32 = (bf16[512,256]{1,0:T(8,128)(2,1)S(1)}, bf16[512,256]{1,0:T(8,128)(2,1)S(1)}, u32[]{:S(2)}, u32[]{:S(2)}) collective-permute-start(bf16[512,256]{1,0:T(8,128)(2,1)S(1)} %collective-permute-done.30), channel_id=1, source_target_pairs={{0,8},{8,16},{16,24},{24,28},{28,20},{20,12},{12,4},{4,0},{1,9},{9... | collective-permute-start | bytes 786440 | tf_op jit(solution)/shard_map/ppermute | solution.py:112
  244.7 13.2 %collective-permute-start.50 = (f16[512,256]{1,0:T(8,128)(2,1)S(1)}, f16[512,256]{1,0:T(8,128)(2,1)S(1)}, u32[]{:S(2)}, u32[]{:S(2)}) collective-permute-start(f16[512,256]{1,0:T(8,128)(2,1)S(1)} %fusion.57), channel_id=1, source_target_pairs={{0,8},{8,16},{16,24},{24,28},{28,20},{20,12},{12,4},{4,0},{1,9},{9... | collective-permute-start | bytes 786440 | tf_op jit(solution)/shard_map/ppermute | solution.py:100
  246.4 13.2 %collective-permute-start.111 = (f16[512,256]{1,0:T(8,128)(2,1)S(1)}, f16[512,256]{1,0:T(8,128)(2,1)S(1)}, u32[]{:S(2)}, u32[]{:S(2)}) collective-permute-start(f16[512,256]{1,0:T(8,128)(2,1)S(1)} %fusion.60), channel_id=1, source_target_pairs={{8,0},{16,8},{24,16},{28,24},{20,28},{12,20},{4,12},{0,4},{9,1},{1... | collective-permute-start | bytes 786440 | tf_op jit(solution)/shard_map/ppermute | solution.py:100
  247.9 13.2 %collective-permute-start.118 = (f16[512,256]{1,0:T(8,128)(2,1)S(1)}, f16[512,256]{1,0:T(8,128)(2,1)S(1)}, u32[]{:S(2)}, u32[]{:S(2)}) collective-permute-start(f16[512,256]{1,0:T(8,128)(2,1)S(1)} %fusion.61), channel_id=1, source_target_pairs={{8,0},{16,8},{24,16},{28,24},{20,28},{12,20},{4,12},{0,4},{9,1},{1... | collective-permute-start | bytes 786440 | tf_op jit(solution)/shard_map/ppermute | solution.py:100
  338.0 13.6 %collective-permute-start.60 = (bf16[512,256]{1,0:T(8,128)(2,1)S(1)}, bf16[512,256]{1,0:T(8,128)(2,1)S(1)}, u32[]{:S(2)}, u32[]{:S(2)}) collective-permute-start(bf16[512,256]{1,0:T(8,128)(2,1)S(1)} %get-tuple-element.362), channel_id=1, source_target_pairs={{0,8},{8,16},{16,24},{24,28},{28,20},{20,12},{12,4},{4,0},{1,9},{9... | collective-permute-start | bytes 786440 | tf_op jit(solution)/shard_map/ppermute | solution.py:112
  339.6 13.2 %collective-permute-start.129 = (bf16[512,256]{1,0:T(8,128)(2,1)S(1)}, bf16[512,256]{1,0:T(8,128)(2,1)S(1)}, u32[]{:S(2)}, u32[]{:S(2)}) collective-permute-start(bf16[512,256]{1,0:T(8,128)(2,1)S(1)} %get-tuple-element.367), channel_id=1, source_target_pairs={{8,0},{16,8},{24,16},{28,24},{20,28},{12,20},{4,12},{0,4},{9,1},{1... | collective-permute-start | bytes 786440 | tf_op jit(solution)/shard_map/ppermute | solution.py:112
  340.6 13.5 %collective-permute-start.128 = (bf16[512,256]{1,0:T(8,128)(2,1)S(1)}, bf16[512,256]{1,0:T(8,128)(2,1)S(1)}, u32[]{:S(2)}, u32[]{:S(2)}) collective-permute-start(bf16[512,256]{1,0:T(8,128)(2,1)S(1)} %get-tuple-element.366), channel_id=1, source_target_pairs={{8,0},{16,8},{24,16},{28,24},{20,28},{12,20},{4,12},{0,4},{9,1},{1... | collective-permute-start | bytes 786440 | tf_op jit(solution)/shard_map/ppermute | solution.py:112
  400.0 14.0 %collective-permute-start.141 = (bf16[512,256]{1,0:T(8,128)(2,1)S(1)}, bf16[512,256]{1,0:T(8,128)(2,1)S(1)}, u32[]{:S(2)}, u32[]{:S(2)}) collective-permute-start(bf16[512,256]{1,0:T(8,128)(2,1)S(1)} %collective-permute-done.139), channel_id=1, source_target_pairs={{8,0},{16,8},{24,16},{28,24},{20,28},{12,20},{4,12},{0,4},{9,1},{1... | collective-permute-start | bytes 786440 | tf_op jit(solution)/shard_map/ppermute | solution.py:112
  402.4 12.0 %collective-permute-start.140 = (bf16[512,256]{1,0:T(8,128)(2,1)S(1)}, bf16[512,256]{1,0:T(8,128)(2,1)S(1)}, u32[]{:S(2)}, u32[]{:S(2)}) collective-permute-start(bf16[512,256]{1,0:T(8,128)(2,1)S(1)} %collective-permute-done.138), channel_id=1, source_target_pairs={{8,0},{16,8},{24,16},{28,24},{20,28},{12,20},{4,12},{0,4},{9,1},{1... | collective-permute-start | bytes 786440 | tf_op jit(solution)/shard_map/ppermute | solution.py:112
  422.3 26.9 %collective-permute-start.145 = (f16[512,256]{1,0:T(8,128)(2,1)S(1)}, f16[512,256]{1,0:T(8,128)(2,1)S(1)}, u32[]{:S(2)}, u32[]{:S(2)}) collective-permute-start(f16[512,256]{1,0:T(8,128)(2,1)S(1)} %fusion.62), channel_id=1, source_target_pairs={{0,8},{8,16},{16,24},{24,28},{28,20},{20,12},{12,4},{4,0},{1,9},{9... | collective-permute-start | bytes 786440 | tf_op jit(solution)/shard_map/ppermute | solution.py:100
  424.9 25.6 %collective-permute-start.152 = (f16[512,256]{1,0:T(8,128)(2,1)S(1)}, f16[512,256]{1,0:T(8,128)(2,1)S(1)}, u32[]{:S(2)}, u32[]{:S(2)}) collective-permute-start(f16[512,256]{1,0:T(8,128)(2,1)S(1)} %fusion.63), channel_id=1, source_target_pairs={{0,8},{8,16},{16,24},{24,28},{28,20},{20,12},{12,4},{4,0},{1,9},{9... | collective-permute-start | bytes 786440 | tf_op jit(solution)/shard_map/ppermute | solution.py:100
  427.6 23.5 %collective-permute-start.159 = (f16[512,256]{1,0:T(8,128)(2,1)S(1)}, f16[512,256]{1,0:T(8,128)(2,1)S(1)}, u32[]{:S(2)}, u32[]{:S(2)}) collective-permute-start(f16[512,256]{1,0:T(8,128)(2,1)S(1)} %fusion.64), channel_id=1, source_target_pairs={{8,0},{16,8},{24,16},{28,24},{20,28},{12,20},{4,12},{0,4},{9,1},{1... | collective-permute-start | bytes 786440 | tf_op jit(solution)/shard_map/ppermute | solution.py:100
  440.5 13.1 %collective-permute-start.166 = (f16[512,256]{1,0:T(8,128)(2,1)S(1)}, f16[512,256]{1,0:T(8,128)(2,1)S(1)}, u32[]{:S(2)}, u32[]{:S(2)}) collective-permute-start(f16[512,256]{1,0:T(8,128)(2,1)S(1)} %fusion.65), channel_id=1, source_target_pairs={{8,0},{16,8},{24,16},{28,24},{20,28},{12,20},{4,12},{0,4},{9,1},{1... | collective-permute-start | bytes 786440 | tf_op jit(solution)/shard_map/ppermute | solution.py:100
  451.0 12.4 %collective-permute-start.153 = (f16[512,256]{1,0:T(8,128)(2,1)S(1)}, f16[512,256]{1,0:T(8,128)(2,1)S(1)}, u32[]{:S(2)}, u32[]{:S(2)}) collective-permute-start(f16[512,256]{1,0:T(8,128)(2,1)S(1)} %multiply_convert_fusion.17), channel_id=1, source_target_pairs={{0,8},{8,16},{16,24},{24,28},{28,20},{20,12},{12,4},{4,0},{1,9},{9... | collective-permute-start | bytes 786440 | tf_op jit(solution)/shard_map/ppermute | solution.py:100
  451.6 12.0 %collective-permute-start.160 = (f16[512,256]{1,0:T(8,128)(2,1)S(1)}, f16[512,256]{1,0:T(8,128)(2,1)S(1)}, u32[]{:S(2)}, u32[]{:S(2)}) collective-permute-start(f16[512,256]{1,0:T(8,128)(2,1)S(1)} %multiply_convert_fusion.11), channel_id=1, source_target_pairs={{8,0},{16,8},{24,16},{28,24},{20,28},{12,20},{4,12},{0,4},{9,1},{1... | collective-permute-start | bytes 786440 | tf_op jit(solution)/shard_map/ppermute | solution.py:100
  454.1 12.3 %collective-permute-start.167 = (f16[512,256]{1,0:T(8,128)(2,1)S(1)}, f16[512,256]{1,0:T(8,128)(2,1)S(1)}, u32[]{:S(2)}, u32[]{:S(2)}) collective-permute-start(f16[512,256]{1,0:T(8,128)(2,1)S(1)} %multiply_convert_fusion.5), channel_id=1, source_target_pairs={{8,0},{16,8},{24,16},{28,24},{20,28},{12,20},{4,12},{0,4},{9,1},{1... | collective-permute-start | bytes 786440 | tf_op jit(solution)/shard_map/ppermute | solution.py:100
  (148 other events, 1282.8 us)

commit v2 on v1

--- a/solution.py
+++ b/solution.py
@@ -21,17 +21,20 @@
     return [2 * q if q < size // 2 else 2 * (size - 1 - q) + 1 for q in range(size)]
 
 
+def stages(size):
+    return size.bit_length() - 1
+
+
 def make_body(rows_size, cols_size):
     order = ring_order(rows_size)
     up = [(order[q], order[(q + 1) % rows_size]) for q in range(rows_size)]
     down = [(b, a) for a, b in up]
     perms = (up, down)
 
-    def total(x, axis, size):
-        step = 1
-        while step < size:
-            x = x + lax.ppermute(x, axis, [(i, i ^ step) for i in range(size)])
-            step *= 2
+    def total(x):
+        for stage in range(stages(rows_size)):
+            sent = lax.ppermute(x, "rows", [(i, i ^ (1 << stage)) for i in range(rows_size)])
+            x = x + sent
         return x
 
     def per_device(margins, subset_masks, ridge_param):
@@ -55,7 +58,7 @@
             if step:
                 sent = lax.ppermute(sent, "cols", [(i, i ^ step) for i in range(cols_size)])
             l1 = sent if l1 is None else l1 + sent
-        target_bound = jnp.maximum(total(l1, "rows", rows_size) * 1.01, 1e-30)
+        target_bound = jnp.maximum(total(l1) * 1.01, 1e-30)
 
         regrouped = jnp.zeros((local_subsets, columns), margins.dtype)
         for step in range(cols_size):
@@ -126,37 +129,40 @@
             [group_of(regrouped, g) for g in groups], [group_of(target_bound, g) for g in groups],
             early=2,
         )
-        first_norms = [total(column_sum(t * t), "rows", rows_size) for t in target]
+        first_norms = [total(column_sum(target[g] * target[g])) for g in groups]
         lows = [t.astype(jnp.bfloat16) for t in target]
+        bound_norms = lax.optimization_barrier(first_norms)
+        first_norms = lax.optimization_barrier(bound_norms)
         fitted0 = gather_times(lows)
         fitted_low = [f.astype(jnp.bfloat16) for f in fitted0]
         curvature = [
             total(
                 column_sum(fitted0[g] * fitted_low[g].astype(jnp.float32))
                 + ridge_param * column_sum(lows[g].astype(jnp.float32) * target[g]),
-                "rows", rows_size,
             )
             for g in groups
         ]
         gain = 1.02 * subsets * float(n) ** 0.5
         image = scatter_sums(
-            fitted_low, [jnp.maximum(gain * jnp.sqrt(v), 1e-30) for v in first_norms]
+            fitted_low, [jnp.maximum(gain * jnp.sqrt(v), 1e-30) for v in bound_norms]
         )
         alpha0 = [first_norms[g] / curvature[g] for g in groups]
         residual = [
             target[g] - alpha0[g] * (image[g] + ridge_param * target[g]) for g in groups
         ]
-        norm1 = [total(column_sum(r * r), "rows", rows_size) for r in residual]
+        residual, lows = lax.optimization_barrier(
+            (residual, [r.astype(jnp.bfloat16) for r in residual])
+        )
+        norm1 = [total(column_sum(residual[g] * residual[g])) for g in groups]
         beta = [norm1[g] / first_norms[g] for g in groups]
         direction = [residual[g] + beta[g] * target[g] for g in groups]
-        fresh = gather_times([r.astype(jnp.bfloat16) for r in residual])
+        fresh = gather_times(lows)
         fitted1 = [fresh[g] + beta[g] * fitted0[g] for g in groups]
         fitted_low = [f.astype(jnp.bfloat16) for f in fitted1]
         curvature = [
             total(
                 column_sum(fitted1[g] * fitted_low[g].astype(jnp.float32))
                 + ridge_param * column_sum(direction[g] * direction[g]),
-                "rows", rows_size,
             )
             for g in groups
         ]
@@ -172,7 +178,7 @@
             residual[g] - alpha1[g] * (image[g] + ridge_param * direction[g]) for g in groups
         ]
         last = jnp.concatenate([column_sum(r * r) for r in residual], axis=1)
-        last = total(last, "rows", rows_size)
+        last = total(last)
         ratio = last / jnp.concatenate(first_norms, axis=1)
         return weights, jnp.sqrt(ratio).reshape(columns)
 

time: 524 us -> 529 us (level)
  waiting for transfers between devices: 197 us -> 219 us
  starting transfers between devices: 200 us -> 183 us
    ppermute x30, waiting for transfers between devices: 36.6 us -> 72.5 us  [total(): lax.ppermute(x, 'rows', [(i, i ^ 1 << stage) for i in range(rows_size)])]
    ppermute x56, waiting for transfers between devices: 72.5 us -> 58.8 us  [gather_times(): following[g, c] = lax.ppermute(held[g, c], 'rows', perms[g])]
    ppermute x30, starting transfers between devices: 42.6 us -> 29.4 us  [total(): lax.ppermute(x, 'rows', [(i, i ^ 1 << stage) for i in range(rows_size)])]
  transfers between devices with their start and end apart: 176 -> 176, of which waited for: 96 -> 84; matrix products, arithmetic and copies ran while one was open for 20% -> 18% of each run, Pallas kernels for 0% -> 0%
where the time goes in v2:
time: 529 us; the launch traced here: 520 us
  waiting for transfers between devices  219 us (41%)
  starting transfers between devices  183 us (35%)
  matrix products  87.8 us (17%)
  other arithmetic  25.1 us (5%)
    ppermute x84, starting transfers between devices, scatter_sums(): value = lax.ppermute(value, 'rows', perms[g])  89.8 us
    ppermute x84, waiting for transfers between devices, scatter_sums(): value = lax.ppermute(value, 'rows', perms[g])  87.5 us
    ppermute x30, waiting for transfers between devices, total(): lax.ppermute(x, 'rows', [(i, i ^ 1 << stage) for i in range(rows_size)])  72.5 us
    dot_general x96, matrix products, partial(): lax.dot_general(design_rows(b, c, s < early), operands[g], (((0,), (0,)),...  59.4 us
    ppermute x56, waiting for transfers between devices, gather_times(): following[g, c] = lax.ppermute(held[g, c], 'rows', perms[g])  58.8 us
    ppermute x56, starting transfers between devices, gather_times(): following[g, c] = lax.ppermute(held[g, c], 'rows', perms[g])  58.1 us
    ppermute x30, starting transfers between devices, total(): lax.ppermute(x, 'rows', [(i, i ^ 1 << stage) for i in range(rows_size)])  29.4 us
    dot_general x64, matrix products, gather_times(): jnp.dot(design_rows(blocks[j], c), held[g, c], preferred_element_type=jnp...  28.4 us
  transfers between devices with their start and end apart: 176, of which 84 were waited for; matrix products, arithmetic and copies ran while one was open for 18% of the time, Pallas kernels for 0%

profile of v2, /device:TPU:0, one launch (start us, length us, event | category | flops | bytes accessed | tf_op | source)
XLA Modules:
  0.0 519.9 jit_solution(13323728007182873385)
XLA Ops:
  8.9 14.1 %multiply_add_fusion = bf16[1024,8192]{1,0:T(8,128)(2,1)} fusion(bf16[1024,8192]{1,0:T(8,128)(2,1)} %param.4), kind=kLoop, calls=%fused_computation | loop fusion | flops 16777216 | bytes 33554432 | tf_op jit(solution)/shard_map/sub | solution.py:71
  65.3 4.6 collective-permute-done.17
  78.1 3.0 collective-permute-done.18
  112.1 3.1 collective-permute-done.21
  148.7 5.2 collective-permute-done.43
  159.9 5.2 collective-permute-done.45
  171.6 4.7 collective-permute-done.47
  182.9 4.7 collective-permute-done.49
  194.1 4.7 collective-permute-done.51
  204.8 3.3 collective-permute-done.53
  233.8 3.7 collective-permute-done.89
  243.2 3.3 collective-permute-done.59
  247.0 5.4 %collective-permute-start.92 = (f16[512,256]{1,0:T(8,128)(2,1)S(1)}, f16[512,256]{1,0:T(8,128)(2,1)S(1)}, u32[]{:S(2)}, u32[]{:S(2)}) collective-permute-start(f16[512,256]{1,0:T(8,128)(2,1)S(1)} %multiply_convert_fusion.35), channel_id=1, source_target_pairs={{8,0},{16,8},{24,16},{28,24},{20,28},{12,20},{4,12},{0,4},{9,1},{1... | collective-permute-start | bytes 786440 | tf_op jit(solution)/shard_map/ppermute | solution.py:103
  261.0 3.0 collective-permute-done.99
  272.2 3.0 collective-permute-done.100
  278.0 3.3 collective-permute-done.69
  289.3 3.3 collective-permute-done.70
  297.3 3.9 collective-permute-done.71
  307.0 3.4 collective-permute-done.72
  313.6 3.7 collective-permute-done.73
  324.1 8.2 %collective-permute-done.125 = f32[1,256]{1,0:T(1,128)S(1)} collective-permute-done((f32[1,256]{1,0:T(1,128)S(1)}, f32[1,256]{1,0:T(1,128)S(1)}, u32[]{:S(2)}, u32[]{:S(2)}) %collective-permute-start.125) | collective-permute-done | bytes 1056 | tf_op jit(solution)/shard_map/ppermute | solution.py:36
  332.4 3.3 collective-permute-start.129
  337.4 11.3 %collective-permute-done.127 = f32[1,256]{1,0:T(1,128)S(1)} collective-permute-done((f32[1,256]{1,0:T(1,128)S(1)}, f32[1,256]{1,0:T(1,128)S(1)}, u32[]{:S(2)}, u32[]{:S(2)}) %collective-permute-start.127) | collective-permute-done | bytes 1056 | tf_op jit(solution)/shard_map/ppermute | solution.py:36
  355.2 3.7 collective-permute-done.111
  360.9 3.6 collective-permute-done.110
  372.1 3.6 collective-permute-done.112
  403.6 3.2 collective-permute-done.121
  407.2 4.7 collective-permute-done.120
  432.5 9.2 %collective-permute-done.142 = f32[1,256]{1,0:T(1,128)S(1)} collective-permute-done((f32[1,256]{1,0:T(1,128)S(1)}, f32[1,256]{1,0:T(1,128)S(1)}, u32[]{:S(2)}, u32[]{:S(2)}) %collective-permute-start.142) | collective-permute-done | bytes 1056 | tf_op jit(solution)/shard_map/ppermute | solution.py:36
  446.8 7.2 %collective-permute-done.144 = f32[1,256]{1,0:T(1,128)S(1)} collective-permute-done((f32[1,256]{1,0:T(1,128)S(1)}, f32[1,256]{1,0:T(1,128)S(1)}, u32[]{:S(2)}, u32[]{:S(2)}) %collective-permute-start.144) | collective-permute-done | bytes 1056 | tf_op jit(solution)/shard_map/ppermute | solution.py:36
  461.9 5.4 %collective-permute-done.153 = f16[512,256]{1,0:T(8,128)(2,1)S(1)} collective-permute-done((f16[512,256]{1,0:T(8,128)(2,1)S(1)}, f16[512,256]{1,0:T(8,128)(2,1)S(1)}, u32[]{:S(2)}, u32[]{:S(2)}) %collective-permute-start.153) | collective-permute-done | bytes 262176 | tf_op jit(solution)/shard_map/ppermute | solution.py:103
  511.2 3.2 collective-permute-done.174
  (602 shorter events, 361.1 us)
Async XLA Ops:
  2.2 20.8 %collective-permute-start.3 = (f32[1,512]{1,0:T(1,128)S(1)}, f32[1,512]{1,0:T(1,128)S(1)}, u32[]{:S(2)}, u32[]{:S(2)}) collective-permute-start(f32[1,512]{1,0:T(1,128)S(1)} %bitcast.458), channel_id=1, source_target_pairs={{0,1},{1,0},{2,3},{3,2},{4,5},{5,4},{6,7},{7,6},{8,9},{9,8},{10,11... | collective-permute-start | bytes 6152 | tf_op jit(solution)/shard_map/ppermute | solution.py:59
  2.7 20.3 %collective-permute-start.4 = (f32[1,512]{1,0:T(1,128)S(1)}, f32[1,512]{1,0:T(1,128)S(1)}, u32[]{:S(2)}, u32[]{:S(2)}) collective-permute-start(f32[1,512]{1,0:T(1,128)S(1)} %bitcast.457), channel_id=1, source_target_pairs={{0,2},{1,3},{2,0},{3,1},{4,6},{5,7},{6,4},{7,5},{8,10},{9,11},{10,... | collective-permute-start | bytes 6152 | tf_op jit(solution)/shard_map/ppermute | solution.py:59
  5.3 17.7 %collective-permute-start.5 = (f32[1,512]{1,0:T(1,128)S(1)}, f32[1,512]{1,0:T(1,128)S(1)}, u32[]{:S(2)}, u32[]{:S(2)}) collective-permute-start(f32[1,512]{1,0:T(1,128)S(1)} %bitcast.456), channel_id=1, source_target_pairs={{0,3},{1,2},{2,1},{3,0},{4,7},{5,6},{6,5},{7,4},{8,11},{9,10},{10,... | collective-permute-start | bytes 6152 | tf_op jit(solution)/shard_map/ppermute | solution.py:59
  6.7 28.1 %collective-permute-start = (bf16[256,512]{1,0:T(8,128)(2,1)S(1)}, bf16[256,512]{1,0:T(8,128)(2,1)S(1)}, u32[]{:S(2)}, u32[]{:S(2)}) collective-permute-start(bf16[256,512]{1,0:T(8,128)(2,1)S(1)} %get-tuple-element.372), channel_id=1, source_target_pairs={{0,1},{1,0},{2,3},{3,2},{4,5},{5,4},{6,7},{7,6},{8,9},{9,8},{10,11... | collective-permute-start | bytes 786440 | tf_op jit(solution)/shard_map/ppermute | solution.py:68
  6.9 27.9 %collective-permute-start.1 = (bf16[256,512]{1,0:T(8,128)(2,1)S(1)}, bf16[256,512]{1,0:T(8,128)(2,1)S(1)}, u32[]{:S(2)}, u32[]{:S(2)}) collective-permute-start(bf16[256,512]{1,0:T(8,128)(2,1)S(1)} %get-tuple-element.371), channel_id=1, source_target_pairs={{0,2},{1,3},{2,0},{3,1},{4,6},{5,7},{6,4},{7,5},{8,10},{9,11},{10,... | collective-permute-start | bytes 786440 | tf_op jit(solution)/shard_map/ppermute | solution.py:68
  57.3 12.6 %collective-permute-start.17 = (f16[512,256]{1,0:T(8,128)(2,1)S(1)}, f16[512,256]{1,0:T(8,128)(2,1)S(1)}, u32[]{:S(2)}, u32[]{:S(2)}) collective-permute-start(f16[512,256]{1,0:T(8,128)(2,1)S(1)} %fusion.78), channel_id=1, source_target_pairs={{0,8},{8,16},{16,24},{24,28},{28,20},{20,12},{12,4},{4,0},{1,9},{9... | collective-permute-start | bytes 786440 | tf_op jit(solution)/shard_map/ppermute | solution.py:103
  62.3 12.7 %collective-permute-start.35 = (f16[512,256]{1,0:T(8,128)(2,1)S(1)}, f16[512,256]{1,0:T(8,128)(2,1)S(1)}, u32[]{:S(2)}, u32[]{:S(2)}) collective-permute-start(f16[512,256]{1,0:T(8,128)(2,1)S(1)} %fusion.67), channel_id=1, source_target_pairs={{8,0},{16,8},{24,16},{28,24},{20,28},{12,20},{4,12},{0,4},{9,1},{1... | collective-permute-start | bytes 786440 | tf_op jit(solution)/shard_map/ppermute | solution.py:103
  123.3 17.6 %collective-permute-start.75 = (bf16[512,256]{1,0:T(8,128)(2,1)S(1)}, bf16[512,256]{1,0:T(8,128)(2,1)S(1)}, u32[]{:S(2)}, u32[]{:S(2)}) collective-permute-start(bf16[512,256]{1,0:T(8,128)(2,1)S(1)} %get-tuple-element.379), channel_id=1, source_target_pairs={{8,0},{16,8},{24,16},{28,24},{20,28},{12,20},{4,12},{0,4},{9,1},{1... | collective-permute-start | bytes 786440 | tf_op jit(solution)/shard_map/ppermute | solution.py:115
  125.0 18.2 %collective-permute-start.74 = (bf16[512,256]{1,0:T(8,128)(2,1)S(1)}, bf16[512,256]{1,0:T(8,128)(2,1)S(1)}, u32[]{:S(2)}, u32[]{:S(2)}) collective-permute-start(bf16[512,256]{1,0:T(8,128)(2,1)S(1)} %get-tuple-element.378), channel_id=1, source_target_pairs={{8,0},{16,8},{24,16},{28,24},{20,28},{12,20},{4,12},{0,4},{9,1},{1... | collective-permute-start | bytes 786440 | tf_op jit(solution)/shard_map/ppermute | solution.py:115
  140.0 13.8 %collective-permute-start.43 = (bf16[512,256]{1,0:T(8,128)(2,1)S(1)}, bf16[512,256]{1,0:T(8,128)(2,1)S(1)}, u32[]{:S(2)}, u32[]{:S(2)}) collective-permute-start(bf16[512,256]{1,0:T(8,128)(2,1)S(1)} %get-tuple-element.380), channel_id=1, source_target_pairs={{0,8},{8,16},{16,24},{24,28},{28,20},{20,12},{12,4},{4,0},{1,9},{9... | collective-permute-start | bytes 786440 | tf_op jit(solution)/shard_map/ppermute | solution.py:115
  141.4 13.4 %collective-permute-start.77 = (bf16[512,256]{1,0:T(8,128)(2,1)S(1)}, bf16[512,256]{1,0:T(8,128)(2,1)S(1)}, u32[]{:S(2)}, u32[]{:S(2)}) collective-permute-start(bf16[512,256]{1,0:T(8,128)(2,1)S(1)} %collective-permute-done.75), channel_id=1, source_target_pairs={{8,0},{16,8},{24,16},{28,24},{20,28},{12,20},{4,12},{0,4},{9,1},{1... | collective-permute-start | bytes 786440 | tf_op jit(solution)/shard_map/ppermute | solution.py:115
  143.1 14.1 %collective-permute-start.76 = (bf16[512,256]{1,0:T(8,128)(2,1)S(1)}, bf16[512,256]{1,0:T(8,128)(2,1)S(1)}, u32[]{:S(2)}, u32[]{:S(2)}) collective-permute-start(bf16[512,256]{1,0:T(8,128)(2,1)S(1)} %collective-permute-done.74), channel_id=1, source_target_pairs={{8,0},{16,8},{24,16},{28,24},{20,28},{12,20},{4,12},{0,4},{9,1},{1... | collective-permute-start | bytes 786440 | tf_op jit(solution)/shard_map/ppermute | solution.py:115
  225.8 20.6 %collective-permute-start.91 = (f16[512,256]{1,0:T(8,128)(2,1)S(1)}, f16[512,256]{1,0:T(8,128)(2,1)S(1)}, u32[]{:S(2)}, u32[]{:S(2)}) collective-permute-start(f16[512,256]{1,0:T(8,128)(2,1)S(1)} %fusion.60), channel_id=1, source_target_pairs={{8,0},{16,8},{24,16},{28,24},{20,28},{12,20},{4,12},{0,4},{9,1},{1... | collective-permute-start | bytes 786440 | tf_op jit(solution)/shard_map/ppermute | solution.py:103
  226.4 25.9 %collective-permute-start.98 = (f16[512,256]{1,0:T(8,128)(2,1)S(1)}, f16[512,256]{1,0:T(8,128)(2,1)S(1)}, u32[]{:S(2)}, u32[]{:S(2)}) collective-permute-start(f16[512,256]{1,0:T(8,128)(2,1)S(1)} %fusion.61), channel_id=1, source_target_pairs={{8,0},{16,8},{24,16},{28,24},{20,28},{12,20},{4,12},{0,4},{9,1},{1... | collective-permute-start | bytes 786440 | tf_op jit(solution)/shard_map/ppermute | solution.py:103
  231.3 21.6 %collective-permute-start.60 = (f16[512,256]{1,0:T(8,128)(2,1)S(1)}, f16[512,256]{1,0:T(8,128)(2,1)S(1)}, u32[]{:S(2)}, u32[]{:S(2)}) collective-permute-start(f16[512,256]{1,0:T(8,128)(2,1)S(1)} %fusion.58), channel_id=1, source_target_pairs={{0,8},{8,16},{16,24},{24,28},{28,20},{20,12},{12,4},{4,0},{1,9},{9... | collective-permute-start | bytes 786440 | tf_op jit(solution)/shard_map/ppermute | solution.py:103
  239.2 16.3 %collective-permute-start.67 = (f16[512,256]{1,0:T(8,128)(2,1)S(1)}, f16[512,256]{1,0:T(8,128)(2,1)S(1)}, u32[]{:S(2)}, u32[]{:S(2)}) collective-permute-start(f16[512,256]{1,0:T(8,128)(2,1)S(1)} %fusion.59), channel_id=1, source_target_pairs={{0,8},{8,16},{16,24},{24,28},{28,20},{20,12},{12,4},{4,0},{1,9},{9... | collective-permute-start | bytes 786440 | tf_op jit(solution)/shard_map/ppermute | solution.py:103
  253.4 13.2 %collective-permute-start.61 = (f16[512,256]{1,0:T(8,128)(2,1)S(1)}, f16[512,256]{1,0:T(8,128)(2,1)S(1)}, u32[]{:S(2)}, u32[]{:S(2)}) collective-permute-start(f16[512,256]{1,0:T(8,128)(2,1)S(1)} %multiply_convert_fusion.47), channel_id=1, source_target_pairs={{0,8},{8,16},{16,24},{24,28},{28,20},{20,12},{12,4},{4,0},{1,9},{9... | collective-permute-start | bytes 786440 | tf_op jit(solution)/shard_map/ppermute | solution.py:103
  268.4 12.9 %collective-permute-start.69 = (f16[512,256]{1,0:T(8,128)(2,1)S(1)}, f16[512,256]{1,0:T(8,128)(2,1)S(1)}, u32[]{:S(2)}, u32[]{:S(2)}) collective-permute-start(f16[512,256]{1,0:T(8,128)(2,1)S(1)} %multiply_convert_fusion.40), channel_id=1, source_target_pairs={{0,8},{8,16},{16,24},{24,28},{28,20},{20,12},{12,4},{4,0},{1,9},{9... | collective-permute-start | bytes 786440 | tf_op jit(solution)/shard_map/ppermute | solution.py:103
  318.7 30.5 %collective-permute-start.109 = (bf16[512,256]{1,0:T(8,128)(2,1)S(1)}, bf16[512,256]{1,0:T(8,128)(2,1)S(1)}, u32[]{:S(2)}, u32[]{:S(2)}) collective-permute-start(bf16[512,256]{1,0:T(8,128)(2,1)S(1)} %get-tuple-element.375), channel_id=1, source_target_pairs={{0,8},{8,16},{16,24},{24,28},{28,20},{20,12},{12,4},{4,0},{1,9},{9... | collective-permute-start | bytes 786440 | tf_op jit(solution)/shard_map/ppermute | solution.py:115
  319.7 31.5 %collective-permute-start.108 = (bf16[512,256]{1,0:T(8,128)(2,1)S(1)}, bf16[512,256]{1,0:T(8,128)(2,1)S(1)}, u32[]{:S(2)}, u32[]{:S(2)}) collective-permute-start(bf16[512,256]{1,0:T(8,128)(2,1)S(1)} %get-tuple-element.374), channel_id=1, source_target_pairs={{0,8},{8,16},{16,24},{24,28},{28,20},{20,12},{12,4},{4,0},{1,9},{9... | collective-permute-start | bytes 786440 | tf_op jit(solution)/shard_map/ppermute | solution.py:115
  332.4 18.8 %collective-permute-start.129 = (bf16[512,256]{1,0:T(8,128)(2,1)S(1)}, bf16[512,256]{1,0:T(8,128)(2,1)S(1)}, u32[]{:S(2)}, u32[]{:S(2)}) collective-permute-start(bf16[512,256]{1,0:T(8,128)(2,1)S(1)} %get-tuple-element.377), channel_id=1, source_target_pairs={{8,0},{16,8},{24,16},{28,24},{20,28},{12,20},{4,12},{0,4},{9,1},{1... | collective-permute-start | bytes 786440 | tf_op jit(solution)/shard_map/ppermute | solution.py:115
  335.9 17.8 %collective-permute-start.128 = (bf16[512,256]{1,0:T(8,128)(2,1)S(1)}, bf16[512,256]{1,0:T(8,128)(2,1)S(1)}, u32[]{:S(2)}, u32[]{:S(2)}) collective-permute-start(bf16[512,256]{1,0:T(8,128)(2,1)S(1)} %get-tuple-element.376), channel_id=1, source_target_pairs={{8,0},{16,8},{24,16},{28,24},{20,28},{12,20},{4,12},{0,4},{9,1},{1... | collective-permute-start | bytes 786440 | tf_op jit(solution)/shard_map/ppermute | solution.py:115
  351.2 13.3 %collective-permute-start.110 = (bf16[512,256]{1,0:T(8,128)(2,1)S(1)}, bf16[512,256]{1,0:T(8,128)(2,1)S(1)}, u32[]{:S(2)}, u32[]{:S(2)}) collective-permute-start(bf16[512,256]{1,0:T(8,128)(2,1)S(1)} %collective-permute-done.108), channel_id=1, source_target_pairs={{0,8},{8,16},{16,24},{24,28},{28,20},{20,12},{12,4},{4,0},{1,9},{9... | collective-permute-start | bytes 786440 | tf_op jit(solution)/shard_map/ppermute | solution.py:115
  351.3 14.7 %collective-permute-start.131 = (bf16[512,256]{1,0:T(8,128)(2,1)S(1)}, bf16[512,256]{1,0:T(8,128)(2,1)S(1)}, u32[]{:S(2)}, u32[]{:S(2)}) collective-permute-start(bf16[512,256]{1,0:T(8,128)(2,1)S(1)} %collective-permute-done.129), channel_id=1, source_target_pairs={{8,0},{16,8},{24,16},{28,24},{20,28},{12,20},{4,12},{0,4},{9,1},{1... | collective-permute-start | bytes 786440 | tf_op jit(solution)/shard_map/ppermute | solution.py:115
  353.7 13.3 %collective-permute-start.130 = (bf16[512,256]{1,0:T(8,128)(2,1)S(1)}, bf16[512,256]{1,0:T(8,128)(2,1)S(1)}, u32[]{:S(2)}, u32[]{:S(2)}) collective-permute-start(bf16[512,256]{1,0:T(8,128)(2,1)S(1)} %collective-permute-done.128), channel_id=1, source_target_pairs={{8,0},{16,8},{24,16},{28,24},{20,28},{12,20},{4,12},{0,4},{9,1},{1... | collective-permute-start | bytes 786440 | tf_op jit(solution)/shard_map/ppermute | solution.py:115
  399.2 12.7 %collective-permute-start.120 = (bf16[512,256]{1,0:T(8,128)(2,1)S(1)}, bf16[512,256]{1,0:T(8,128)(2,1)S(1)}, u32[]{:S(2)}, u32[]{:S(2)}) collective-permute-start(bf16[512,256]{1,0:T(8,128)(2,1)S(1)} %collective-permute-done.118), channel_id=1, source_target_pairs={{0,8},{8,16},{16,24},{24,28},{28,20},{20,12},{12,4},{4,0},{1,9},{9... | collective-permute-start | bytes 786440 | tf_op jit(solution)/shard_map/ppermute | solution.py:115
  400.1 18.2 %collective-permute-start.141 = (bf16[512,256]{1,0:T(8,128)(2,1)S(1)}, bf16[512,256]{1,0:T(8,128)(2,1)S(1)}, u32[]{:S(2)}, u32[]{:S(2)}) collective-permute-start(bf16[512,256]{1,0:T(8,128)(2,1)S(1)} %collective-permute-done.139), channel_id=1, source_target_pairs={{8,0},{16,8},{24,16},{28,24},{20,28},{12,20},{4,12},{0,4},{9,1},{1... | collective-permute-start | bytes 786440 | tf_op jit(solution)/shard_map/ppermute | solution.py:115
  402.1 16.6 %collective-permute-start.140 = (bf16[512,256]{1,0:T(8,128)(2,1)S(1)}, bf16[512,256]{1,0:T(8,128)(2,1)S(1)}, u32[]{:S(2)}, u32[]{:S(2)}) collective-permute-start(bf16[512,256]{1,0:T(8,128)(2,1)S(1)} %collective-permute-done.138), channel_id=1, source_target_pairs={{8,0},{16,8},{24,16},{28,24},{20,28},{12,20},{4,12},{0,4},{9,1},{1... | collective-permute-start | bytes 786440 | tf_op jit(solution)/shard_map/ppermute | solution.py:115
  426.8 27.2 %collective-permute-start.145 = (f16[512,256]{1,0:T(8,128)(2,1)S(1)}, f16[512,256]{1,0:T(8,128)(2,1)S(1)}, u32[]{:S(2)}, u32[]{:S(2)}) collective-permute-start(f16[512,256]{1,0:T(8,128)(2,1)S(1)} %fusion.62), channel_id=1, source_target_pairs={{0,8},{8,16},{16,24},{24,28},{28,20},{20,12},{12,4},{4,0},{1,9},{9... | collective-permute-start | bytes 786440 | tf_op jit(solution)/shard_map/ppermute | solution.py:103
  427.5 27.6 %collective-permute-start.152 = (f16[512,256]{1,0:T(8,128)(2,1)S(1)}, f16[512,256]{1,0:T(8,128)(2,1)S(1)}, u32[]{:S(2)}, u32[]{:S(2)}) collective-permute-start(f16[512,256]{1,0:T(8,128)(2,1)S(1)} %fusion.63), channel_id=1, source_target_pairs={{0,8},{8,16},{16,24},{24,28},{28,20},{20,12},{12,4},{4,0},{1,9},{9... | collective-permute-start | bytes 786440 | tf_op jit(solution)/shard_map/ppermute | solution.py:103
  432.0 23.7 %collective-permute-start.159 = (f16[512,256]{1,0:T(8,128)(2,1)S(1)}, f16[512,256]{1,0:T(8,128)(2,1)S(1)}, u32[]{:S(2)}, u32[]{:S(2)}) collective-permute-start(f16[512,256]{1,0:T(8,128)(2,1)S(1)} %fusion.64), channel_id=1, source_target_pairs={{8,0},{16,8},{24,16},{28,24},{20,28},{12,20},{4,12},{0,4},{9,1},{1... | collective-permute-start | bytes 786440 | tf_op jit(solution)/shard_map/ppermute | solution.py:103
  445.3 12.9 %collective-permute-start.166 = (f16[512,256]{1,0:T(8,128)(2,1)S(1)}, f16[512,256]{1,0:T(8,128)(2,1)S(1)}, u32[]{:S(2)}, u32[]{:S(2)}) collective-permute-start(f16[512,256]{1,0:T(8,128)(2,1)S(1)} %fusion.65), channel_id=1, source_target_pairs={{8,0},{16,8},{24,16},{28,24},{20,28},{12,20},{4,12},{0,4},{9,1},{1... | collective-permute-start | bytes 786440 | tf_op jit(solution)/shard_map/ppermute | solution.py:103
  (148 other events, 1331.0 us)
